TPU v7x, 32 devices: a 4x4x1 block of a 4x4x8 slice. The times are simulated.
32 devices in a mesh: batch: 1 (over z), col: 4 (over y), row: 8 (over x, core).
Axes of the slice: x: 4, y: 4, z: 1, core: 2. Of those that a mesh axis runs over, the one named last changes fastest.
The devices are a block of a 4x4x8 slice.
Arguments:
- lower_tri: float32 [3072, 3072], P(('batch', 'row'), 'col')
Outputs:
- output: float32 [3072, 3072], P(('batch', 'row'), 'col')
All inputs are finite; a program needn't handle non-finite values.
Results may differ from a plain program's by a relative error of at most 0.001.
Values sent between devices are 32-bit elements.
A program may use at most 768 MiB of HBM per device.

v0:
```python
import jax
import jax.numpy as jnp
from jax import lax
from jax.experimental import pallas as pl
from jax.experimental.pallas import tpu as pltpu
from jax.sharding import PartitionSpec as P

HIGHEST = lax.Precision.HIGHEST
MESH = pl.DeviceIdType.MESH
SIDE = 4
ROUNDS = 6
ORDER = (
    "A0", "T0", "B00", "B01", "T1", "C00", "C01", "A1", "C03", "A2", "B02", "C02", "C05", "C04",
    "D00", "S0", "B10", "B11", "C11", "D01", "C10", "B20", "S1", "B21", "C20", "C21", "C06", "D02",
    "C07", "S2", "B12", "C13", "B22", "C12", "C15", "C14", "C23", "S3", "D10", "C25", "D03", "C22",
    "C17", "C24", "D20", "D11", "C27", "C16", "A4", "A5", "D21", "C26", "D13", "D12", "B40", "B41",
    "P1", "I00", "B50", "B51", "I01", "D22", "D23", "C41", "C40", "C51", "A3", "B42", "C43", "C50",
    "P0", "P2", "G100", "C42", "C45", "G101", "B52", "C44", "C53", "I10", "B30", "B31", "C52", "I11",
    "C31", "C54", "C55", "D40", "G200", "C30", "C47", "D41", "C46", "G201", "B32", "D50", "G210", "C56",
    "C57", "D42", "D51", "G211", "C32", "C33", "C34", "C35", "I20", "D43", "D52", "I21", "C37", "D30",
    "D53", "P4", "G310", "C36", "D31", "D32", "G311", "P5", "D33", "H32", "P3", "H30", "I30", "I31",
)


def dot_nn(a, b):
    return lax.dot_general(a, b, (((1,), (0,)), ((), ())), precision=HIGHEST, preferred_element_type=jnp.float32)


def dot_nt(a, b):
    return lax.dot_general(a, b, (((1,), (1,)), ((), ())), precision=HIGHEST, preferred_element_type=jnp.float32)


def leaf_inverse(leaf, inv):
    order = leaf.shape[0]
    part = 128
    count = order // part
    rows = lax.broadcasted_iota(jnp.int32, (part, part), 0)
    cols = lax.broadcasted_iota(jnp.int32, (part, part), 1)

    def blk(i, j):
        return leaf[part * i : part * (i + 1), part * j : part * (j + 1)]

    diag = [blk(q, q) for q in range(count)]
    done = [jnp.where(rows == cols, 1.0 / d, 0.0) for d in diag]

    def merge(level, xs):
        rbit, cbit = rows >> level, cols >> level
        low = (rbit == cbit + 1) & (cbit & 1 == 0)
        prods = [dot_nn(jnp.where(low, blk(q, q), 0.0), x) for q, x in enumerate(xs)]
        return tuple(x - dot_nn(x, t) for x, t in zip(xs, prods))

    done = lax.fori_loop(0, part.bit_length() - 1, merge, tuple(done))
    out = {}
    for i in range(count):
        out[i, i] = done[i]
    for gap in range(1, count):
        for j in range(count - gap):
            i = j + gap
            acc = dot_nn(blk(i, j), out[j, j])
            for k in range(j + 1, i):
                acc = acc + dot_nn(blk(i, k), out[k, j])
            out[i, j] = -dot_nn(out[i, i], acc)
    for n, (i, j) in enumerate((i, j) for j in range(count) for i in range(j, count)):
        inv[n] = out[i, j]


def make_kernel(leaf_n, share, strip):
    wide = 2 * leaf_n
    part = leaf_n // 3
    head = 8
    shifts = (0, SIDE - 1, 1, 2)
    DIRS = (1, -1, 1, -1)

    def kernel(own, out, off, diag, leaf, inv, low, pmat, zmat,
               scat_send, scat_recv, ring_send, ring_recv, pair_send, pair_recv, out_send, out_recv):
        row = lax.axis_index("row")
        y = lax.axis_index("col")
        x = row // 2
        k = row % 2
        me = SIDE * x + y
        def off_of(a, yy):
            return off.at[a * (a - 1) // 2 + yy]

        def dev(cx, cy, core):
            return {"row": 2 * cx + core, "col": cy}

        barrier = pltpu.get_barrier_semaphore()

        def greet(t, carry):
            @pl.when(t != row * SIDE + y)
            def _():
                pl.semaphore_signal(barrier, inc=1, device_id={"row": t // SIDE, "col": t % SIDE}, device_id_type=MESH)
            return carry

        lax.fori_loop(0, 2 * SIDE * SIDE, greet, 0)
        pl.semaphore_wait(barrier, 2 * SIDE * SIDE - 1)

        def scatter(src_of, dst_of, cond, core, send_row, sem, first=0, last=SIDE * SIDE):
            @pl.when(cond)
            def _():
                def body(m, carry):
                    src, dst = src_of(m), dst_of(m)
                    here = (m == me) & (core == k)

                    @pl.when(here)
                    def _():
                        pltpu.make_async_copy(src, dst, scat_recv.at[sem]).start()

                    @pl.when(jnp.logical_not(here))
                    def _():
                        pltpu.make_async_remote_copy(
                            src_ref=src, dst_ref=dst, send_sem=scat_send.at[send_row], recv_sem=scat_recv.at[sem],
                            device_id=dev(m // SIDE, m % SIDE, core), device_id_type=MESH).start()
                    return carry

                lax.fori_loop(first, last, body, 0)

        PARTS = {0: (0, head), 1: (head, strip - head), 2: (0, strip)}

        def strip_rows(m, core, part):
            start, count = PARTS[part]
            return pl.ds(pl.multiple_of(leaf_n * core + strip * m, 8) + start, count)

        def off_src(part):
            return lambda m: own.at[strip_rows(m, 0, part), :]

        def off_dst(a, yy, part):
            return lambda m: off_of(a, yy).at[strip_rows(m, k, part), :]

        def off_sem(a, yy, part):
            return {1: 0, 2: 1 + yy, 3: 6 + yy}[a] + (3 if part == 1 else 0)

        def scatter_off(a, part, *span):
            for yy in range(a):
                scatter(off_src(part), off_dst(a, yy, part), (x == a) & (y == yy), k, part % 2, off_sem(a, yy, part),
                        *span)

        def band(m):
            return pl.ds(pl.multiple_of(8 * m, 8), 8)

        def low_at(a):
            return 6 * SIDE + 9 * (a % 2)

        def scatter_low(a):
            core = a // 2
            scatter(lambda m: low.at[:, band(m), :], lambda m: diag.at[core, low_at(a) : low_at(a) + 9, band(m), :],
                    (x == a) & (y == a) & (k == 1), core, 1, 13 + a % 2)

        def scatter_inv(a):
            scatter(lambda m: inv.at[:, band(m), :], lambda m: diag.at[k, 6 * a : 6 * (a + 1), band(m), :],
                    (x == a) & (y == a), k, 0, 9 + a)

        def landed(dst, src_like, sem, is_source):
            @pl.when(is_source)
            def _():
                pltpu.make_async_copy(src_like, dst, scat_recv.at[sem]).wait()

            @pl.when(jnp.logical_not(is_source))
            def _():
                pltpu.make_async_remote_copy(
                    src_ref=src_like, dst_ref=dst, send_sem=scat_send.at[0], recv_sem=scat_recv.at[sem],
                    device_id=dev(x, y, 1 - k), device_id_type=MESH).wait_recv()

        def landed_off(a, places, part):
            for yy in places:
                landed(off_dst(a, yy, part)(me), off_src(part)(me), off_sem(a, yy, part), (x == a) & (y == yy))

        def landed_diag():
            for a in range(SIDE):
                landed(diag.at[k, 6 * a : 6 * (a + 1), band(me), :], inv.at[:, band(me), :], 9 + a, (x == a) & (y == a))
            for q in range(2):
                a = 2 * k + q
                landed(diag.at[k, low_at(q) : low_at(q) + 9, band(me), :], low.at[:, band(me), :], 13 + q,
                       (x == a) & (y == a) & (k == 1))

        def relative(du, dv):
            cx = (x + du + k * (dv - du)) % SIDE
            cy = (y + dv + k * (du - dv)) % SIDE
            return cx, cy, SIDE * cx + cy

        chips = {(du, dv): relative(du, dv) for du in range(SIDE) for dv in range(SIDE)}

        def chip_at(du, dv):
            return chips[du % SIDE, dv % SIDE]

        def piece(rnd, core, chip):
            m = chip[2]
            if rnd == 1:
                return diag.at[core, :, band(m), :]
            if rnd >= 3:
                return off.at[rnd, strip_rows(m, core, 2), :]
            return off.at[0:3, strip_rows(m, core, rnd // 2), :]

        def strips(rnd, n):
            if rnd == 1:
                return diag.at[0, :, 0 : 8 * n, :]
            if rnd >= 3:
                return off.at[rnd, 0 : strip * n, :]
            return off.at[0:3, 0 : PARTS[rnd // 2][1] * n, :]

        def sent(ref, sem):
            pltpu.make_async_remote_copy(
                src_ref=ref, dst_ref=ref, send_sem=sem, recv_sem=scat_recv.at[0],
                device_id=dev(x, y, 1 - k), device_id_type=MESH).wait_send()

        def ring_copy(rnd, du, dv, tu, tv, idx):
            ref = piece(rnd, k, chip_at(du, dv))
            return pltpu.make_async_remote_copy(
                src_ref=ref, dst_ref=ref, send_sem=ring_send.at[rnd], recv_sem=ring_recv.at[rnd, idx],
                device_id=dev(*chip_at(tu, tv)[:2], k), device_id_type=MESH)

        def ring_start(*args):
            ring_copy(*args).start()

        def ring_wait(rnd, du, dv, idx):
            ring_copy(rnd, du, dv, 0, 1, idx).wait_recv()

        def pair_start(rnd, g, dv):
            ref = piece(rnd, k, chip_at(shifts[g], dv))
            pltpu.make_async_remote_copy(
                src_ref=ref, dst_ref=ref, send_sem=pair_send.at[rnd], recv_sem=pair_recv.at[rnd],
                device_id=dev(x, y, 1 - k), device_id_type=MESH).start()

        def spread(rnd, g):
            ring_start(rnd, shifts[g], 0, 0, 1, 3 + 3 * g)
            ring_start(rnd, shifts[g], 0, 0, -1, 4 + 3 * g)
            pair_start(rnd, g, 0)

        def stage_a(rnd):
            arrive(rnd)
            ring_start(rnd, 0, 0, 1, 0, 0)
            ring_start(rnd, 0, 0, -1, 0, 1)
            spread(rnd, 0)

        def stage_b(rnd, j):
            ring_wait(rnd, (-1, 1, 2)[j], 0, j)
            if j == 0 and rnd % 2 == 0:
                ring_start(rnd, -1, 0, 1, 0, 2)
            if j == 1 and rnd % 2 == 1:
                ring_start(rnd, 1, 0, -1, 0, 2)
            spread(rnd, j + 1)

        def stage_c(rnd, j):
            g, back = j // 2, j % 2
            from_v = 1 if back else -1
            ring_wait(rnd, shifts[g], from_v, 3 + 3 * g + back)
            if DIRS[g] == -from_v:
                ring_start(rnd, shifts[g], from_v, 0, -from_v, 5 + 3 * g)
            pair_start(rnd, g, from_v)

        def stage_d(rnd, g):
            ring_wait(rnd, shifts[g], 2, 5 + 3 * g)
            pair_start(rnd, g, 2)

        def pair_done(rnd):
            ref = strips(rnd, SIDE * SIDE)
            pltpu.make_async_remote_copy(
                src_ref=ref, dst_ref=ref, send_sem=pair_send.at[rnd], recv_sem=pair_recv.at[rnd],
                device_id=dev(x, y, 1 - k), device_id_type=MESH).wait_recv()

        def column(core, start, count):
            col = diag[core, pl.ds(start, count)].reshape(part * count, part)
            return col if count == 3 else jnp.concatenate([jnp.zeros((part * (3 - count), part), jnp.float32), col], axis=0)

        def low_of(a):
            return jnp.concatenate([column(a // 2, low_at(a) + 3 * c, 3) for c in range(3)], axis=1)

        def inv_of(a, h):
            return jnp.concatenate([column(h, 6 * a + n, c) for n, c in ((0, 3), (3, 2), (5, 1))], axis=1)

        j0 = leaf_n * row + share * y
        rowi = lax.broadcasted_iota(jnp.int32, (share, leaf_n), 0)
        coli = lax.broadcasted_iota(jnp.int32, (share, leaf_n), 1)

        def leaf_cols(i):
            return pl.ds(pl.multiple_of(leaf_n * i, 128), leaf_n)

        begun = set()

        def subtract(a, kk, h):
            place = leaf_cols(2 * a + h)
            rows = pl.ds(pl.multiple_of(leaf_n * h, 8), leaf_n)
            acc = dot_nt(pmat[:, wide * kk : wide * (kk + 1)], off_of(a, kk)[rows, :])
            pmat[:, place] = pmat[:, place] + acc if a in begun else acc

        def subtract_both(a, kk):
            def body(h, carry):
                subtract(a, kk, h)
                return carry

            lax.fori_loop(0, 2, body, 0)
            begun.add(a)

        def subtract_one(a, kk, h):
            subtract(a, kk, h)
            if h:
                begun.add(a)

        def finish(a, h):
            lo = wide * a + leaf_n * h
            rest = jnp.where(rowi + j0 == coli + lo, 1.0, 0.0)
            if a:
                rest = rest - pmat[:, lo : lo + leaf_n]
            if h:
                rest = rest - dot_nt(pmat[:, lo - leaf_n : lo], low_of(a))
            pmat[:, lo : lo + leaf_n] = dot_nt(rest, inv_of(a, h))

        def out_at(src_y, h):
            return out.at[pl.ds(pl.multiple_of(share * src_y, 8), share), leaf_cols(h)]

        def out_copy(a, h, src_y, yy):
            return pltpu.make_async_remote_copy(
                src_ref=zmat.at[:, leaf_cols(2 * a + h)], dst_ref=out_at(src_y, h),
                send_sem=out_send.at[2 * a + h], recv_sem=out_recv.at[src_y, h],
                device_id={"row": row, "col": yy}, device_id_type=MESH)

        def ship(a, h, wait):
            @pl.when(y == a)
            def _():
                c = pltpu.make_async_copy(zmat.at[:, leaf_cols(2 * a + h)], out_at(y, h), out_send.at[2 * a + h])
                c.wait() if wait else c.start()

            @pl.when(y != a)
            def _():
                c = out_copy(a, h, y, a)
                c.wait_send() if wait else c.start()

        def backward(a):
            def rest(h):
                r = pmat[:, leaf_cols(2 * a + h)]
                for b in range(a + 1, SIDE):
                    blk = off_of(b, a)[:, leaf_n * h : leaf_n * (h + 1)]
                    r = r - dot_nn(zmat[:, wide * b : wide * (b + 1)], blk)
                return r

            z1 = dot_nn(rest(1), inv_of(a, 1))
            zmat[:, leaf_cols(2 * a + 1)] = z1
            ship(a, 1, False)
            zmat[:, leaf_cols(2 * a)] = dot_nn(rest(0) - dot_nn(z1, low_of(a)), inv_of(a, 0))
            ship(a, 0, False)

        with jax.named_scope("scatter_send"):
            for a in (1, 2):
                scatter_off(a, 0)

            @pl.when((x == y) & (k == 1))
            def _():
                for c in range(3):
                    for r in range(3):
                        low[3 * c + r] = own[part * r : part * (r + 1), part * c : part * (c + 1)]

            for a in range(SIDE):
                scatter_low(a)

        with jax.named_scope("leaf"):
            @pl.when((x == y) & (k == 0))
            def _():
                leaf[...] = own[:, :leaf_n]

            @pl.when((x == y) & (k == 1))
            def _():
                leaf[...] = own[:, leaf_n:]

            @pl.when(x == y)
            def _():
                leaf_inverse(leaf, inv)

            for a in range(SIDE):
                scatter_inv(a)

        def step(name, fn, *args):
            with jax.named_scope(name):
                fn(*args)

        def arrive(rnd):
            if rnd == 1:
                landed_diag()
            elif rnd < 3:
                landed_off(1, (0,), rnd // 2)
                landed_off(2, (0, 1), rnd // 2)
            else:
                landed_off(3, (rnd - 3,), 2)

        def scatter_rest(q):
            for a in (1, 2):
                scatter_off(a, 1, 8 * q, 8 * (q + 1))

        stages = {"A": stage_a, "B": stage_b, "C": stage_c, "D": stage_d, "P": pair_done, "G": subtract_one, "H": subtract_both, "I": finish,
                  "S": lambda q: scatter_off(3, 2, SIDE * q, SIDE * (q + 1)), "T": scatter_rest}
        for token in ORDER:
            step(token, stages[token[0]], *(int(d) for d in token[1:]))
        for a in range(SIDE - 1, -1, -1):
            step(f"backward{a}", backward, a)

        for rnd in range(ROUNDS):
            sent(strips(rnd, SIDE * SIDE - 1), ring_send.at[rnd])
            sent(strips(rnd, SIDE * SIDE), pair_send.at[rnd])
        others = SIDE * SIDE - 1
        for p in range(2):
            @pl.when((y < x) & (x < 3))
            def _():
                sent(off.at[0, 0 : PARTS[p][1] * others, :], scat_send.at[p])

        @pl.when((y < x) & (x == 3))
        def _():
            sent(off.at[0, 0 : strip * others, :], scat_send.at[0])

        @pl.when(x == y)
        def _():
            sent(inv.at[:, 0 : 8 * others, :], scat_send.at[0])

        for core in range(2):
            @pl.when((x == y) & (k == 1) & (x // 2 == core))
            def _():
                sent(low.at[:, 0 : 8 * (others + 1 - core), :], scat_send.at[1])
        for a in range(SIDE):
            for h in range(2):
                ship(a, h, True)
        for yy in range(SIDE):
            @pl.when(y != yy)
            def _():
                for h in range(2):
                    out_copy(0, h, yy, y).wait_recv()

    return kernel


def solution(mesh):
    count_c = mesh.shape["col"]

    def local_fn(block):
        leaf_n, wide = block.shape
        share = leaf_n // count_c
        strip = leaf_n // (SIDE * SIDE)
        order = wide * count_c
        f32 = jnp.float32
        return pl.pallas_call(
            make_kernel(leaf_n, share, strip),
            out_shape=jax.ShapeDtypeStruct(block.shape, f32),
            in_specs=[pl.BlockSpec(memory_space=pltpu.VMEM)],
            out_specs=pl.BlockSpec(memory_space=pl.ANY),
            scratch_shapes=[
                pltpu.VMEM((6, wide, wide), f32),
                pltpu.VMEM((2, 42, leaf_n // 3, leaf_n // 3), f32),
                pltpu.VMEM((leaf_n, leaf_n), f32),
                pltpu.VMEM((6, leaf_n // 3, leaf_n // 3), f32),
                pltpu.VMEM((9, leaf_n // 3, leaf_n // 3), f32),
                pltpu.VMEM((share, order), f32),
                pltpu.VMEM((share, order), f32),
                pltpu.SemaphoreType.DMA((2,)),
                pltpu.SemaphoreType.DMA((15,)),
                pltpu.SemaphoreType.DMA((ROUNDS,)),
                pltpu.SemaphoreType.DMA((ROUNDS, 15)),
                pltpu.SemaphoreType.DMA((ROUNDS,)),
                pltpu.SemaphoreType.DMA((ROUNDS,)),
                pltpu.SemaphoreType.DMA((2 * SIDE,)),
                pltpu.SemaphoreType.DMA((SIDE, 2)),
            ],
            compiler_params=pltpu.CompilerParams(
                collective_id=0, has_side_effects=True, vmem_limit_bytes=60 * 2**20),
            name="spd_inverse",
        )(block)

    spec = P(("batch", "row"), "col")
    return jax.shard_map(local_fn, mesh=mesh, in_specs=(spec,), out_specs=spec, check_vma=False)
```

profile of v0, /device:TPU:96, one launch (start us, length us, event | category | flops | bytes accessed | tf_op | source)
XLA Modules:
  0.0 121.5 jit_solution(4392290501291661283)
XLA Ops:
  0.0 119.2 %spd_inverse.1 = f32[384,768]{1,0:T(8,128)} custom-call(f32[384,768]{1,0:T(8,128)} %own.1), custom_call_target="tpu_custom_call" | custom-call | tf_op jit(solution)/shard_map/spd_inverse/pallas_call | solution.py:437
  119.2 2.4 %copy.3 = f32[384,768]{1,0:T(8,128)} copy(f32[384,768]{1,0:T(8,128)} %spd_inverse.1) | data formatting | bytes 2359296
where the time goes:
time: 123 us; the launch traced here: 122 us
  Pallas kernels  119 us (97%)
  local copies, waits for them, and re-layouts  2.36 us (2%)
    pallas_call x1, Pallas kernels, local_fn(): pl.pallas_call(make_kernel(leaf_n, share, strip), out_shape=jax.ShapeDtyp...  119 us

commit v1 on v0

--- a/solution.py
+++ b/solution.py
@@ -8,17 +8,19 @@
 HIGHEST = lax.Precision.HIGHEST
 MESH = pl.DeviceIdType.MESH
 SIDE = 4
-ROUNDS = 6
+ROUNDS = 7
 ORDER = (
-    "A0", "T0", "B00", "B01", "T1", "C00", "C01", "A1", "C03", "A2", "B02", "C02", "C05", "C04",
-    "D00", "S0", "B10", "B11", "C11", "D01", "C10", "B20", "S1", "B21", "C20", "C21", "C06", "D02",
-    "C07", "S2", "B12", "C13", "B22", "C12", "C15", "C14", "C23", "S3", "D10", "C25", "D03", "C22",
-    "C17", "C24", "D20", "D11", "C27", "C16", "A4", "A5", "D21", "C26", "D13", "D12", "B40", "B41",
-    "P1", "I00", "B50", "B51", "I01", "D22", "D23", "C41", "C40", "C51", "A3", "B42", "C43", "C50",
-    "P0", "P2", "G100", "C42", "C45", "G101", "B52", "C44", "C53", "I10", "B30", "B31", "C52", "I11",
-    "C31", "C54", "C55", "D40", "G200", "C30", "C47", "D41", "C46", "G201", "B32", "D50", "G210", "C56",
-    "C57", "D42", "D51", "G211", "C32", "C33", "C34", "C35", "I20", "D43", "D52", "I21", "C37", "D30",
-    "D53", "P4", "G310", "C36", "D31", "D32", "G311", "P5", "D33", "H32", "P3", "H30", "I30", "I31",
+    "A0", "T0", "B00", "B01", "T1", "C00", "C01", "A1", "A2", "C03", "A6", "B02", "C02", "C05",
+    "C04", "D00", "B10", "B11", "S0", "C11", "B20", "B21", "C21", "D01", "C10", "B60", "B61", "S1",
+    "C20", "C61", "B22", "C60", "C06", "C07", "B12", "S2", "D02", "B62", "C13", "C12", "C15", "C23",
+    "C25", "C14", "S3", "C22", "C63", "C24", "C65", "C27", "D10", "D03", "C62", "C64", "C17", "D20",
+    "C26", "A4", "C67", "D60", "D11", "D21", "C16", "A5", "D61", "B40", "B41", "C66", "D23", "D12",
+    "B50", "B51", "A3", "D13", "D22", "C41", "B42", "P1", "I00", "D63", "D62", "I01", "C51", "C40",
+    "P0", "P2", "G100", "B52", "C50", "B30", "C43", "G101", "B31", "C42", "C44", "C45", "I10", "C52",
+    "C53", "I11", "C54", "C55", "C31", "C30", "P6", "G200", "C46", "C47", "G201", "C56", "C57", "B32",
+    "D40", "G210", "D50", "C32", "C33", "D41", "G211", "D51", "C34", "C35", "I20", "D42", "D43", "I21",
+    "D52", "D53", "D30", "C37", "P4", "G310", "C36", "D31", "D32", "G311", "P5", "D33", "H32", "P3",
+    "H30", "I30", "I31",
 )
 
 
@@ -183,20 +185,24 @@
         def chip_at(du, dv):
             return chips[du % SIDE, dv % SIDE]
 
+        HEADS = {0: (0, 3, 0), 2: (0, 1, 1), 6: (1, 3, 1)}
+
         def piece(rnd, core, chip):
             m = chip[2]
             if rnd == 1:
                 return diag.at[core, :, band(m), :]
-            if rnd >= 3:
-                return off.at[rnd, strip_rows(m, core, 2), :]
-            return off.at[0:3, strip_rows(m, core, rnd // 2), :]
+            if rnd in HEADS:
+                lo, hi, part = HEADS[rnd]
+                return off.at[lo:hi, strip_rows(m, core, part), :]
+            return off.at[rnd, strip_rows(m, core, 2), :]
 
         def strips(rnd, n):
             if rnd == 1:
                 return diag.at[0, :, 0 : 8 * n, :]
-            if rnd >= 3:
-                return off.at[rnd, 0 : strip * n, :]
-            return off.at[0:3, 0 : PARTS[rnd // 2][1] * n, :]
+            if rnd in HEADS:
+                lo, hi, part = HEADS[rnd]
+                return off.at[lo:hi, 0 : PARTS[part][1] * n, :]
+            return off.at[rnd, 0 : strip * n, :]
 
         def sent(ref, sem):
             pltpu.make_async_remote_copy(
@@ -375,9 +381,12 @@
         def arrive(rnd):
             if rnd == 1:
                 landed_diag()
-            elif rnd < 3:
-                landed_off(1, (0,), rnd // 2)
-                landed_off(2, (0, 1), rnd // 2)
+            elif rnd in HEADS:
+                lo, hi, part = HEADS[rnd]
+                if lo == 0:
+                    landed_off(1, (0,), part)
+                if hi == 3:
+                    landed_off(2, (0, 1), part)
             else:
                 landed_off(3, (rnd - 3,), 2)
 

time: 123 us -> 123 us (level)
  the two profiles are of different devices: /device:TPU:96 before, /device:TPU:100 now
where the time goes in v1:
time: 123 us; the launch traced here: 122 us
  Pallas kernels  120 us (98%)
  local copies, waits for them, and re-layouts  2.36 us (2%)
    pallas_call x1, Pallas kernels, local_fn(): pl.pallas_call(make_kernel(leaf_n, share, strip), out_shape=jax.ShapeDtyp...  120 us

profile of v1, /device:TPU:100, one launch (start us, length us, event | category | flops | bytes accessed | tf_op | source)
XLA Modules:
  0.0 122.4 jit_solution(12842846735540119459)
XLA Ops:
  0.0 120.1 %spd_inverse.1 = f32[384,768]{1,0:T(8,128)} custom-call(f32[384,768]{1,0:T(8,128)} %own.1), custom_call_target="tpu_custom_call" | custom-call | tf_op jit(solution)/shard_map/spd_inverse/pallas_call | solution.py:446
  120.1 2.4 %copy.3 = f32[384,768]{1,0:T(8,128)} copy(f32[384,768]{1,0:T(8,128)} %spd_inverse.1) | data formatting | bytes 2359296

commit v2 on v1

--- a/solution.py
+++ b/solution.py
@@ -73,8 +73,8 @@
     shifts = (0, SIDE - 1, 1, 2)
     DIRS = (1, -1, 1, -1)
 
-    def kernel(own, out, off, diag, leaf, inv, low, pmat, zmat,
-               scat_send, scat_recv, ring_send, ring_recv, pair_send, pair_recv, out_send, out_recv):
+    def kernel(block, out, own, off, diag, leaf, inv, low, pmat, zmat,
+               scat_send, scat_recv, ring_send, ring_recv, pair_send, pair_recv, out_send, out_recv, load_sem):
         row = lax.axis_index("row")
         y = lax.axis_index("col")
         x = row // 2
@@ -86,6 +86,9 @@
         def dev(cx, cy, core):
             return {"row": 2 * cx + core, "col": cy}
 
+        load = pltpu.make_async_copy(block, own, load_sem.at[0])
+        load.start()
+
         barrier = pltpu.get_barrier_semaphore()
 
         def greet(t, carry):
@@ -95,6 +98,7 @@
             return carry
 
         lax.fori_loop(0, 2 * SIDE * SIDE, greet, 0)
+        load.wait()
         pl.semaphore_wait(barrier, 2 * SIDE * SIDE - 1)
 
         def scatter(src_of, dst_of, cond, core, send_row, sem, first=0, last=SIDE * SIDE):
@@ -446,9 +450,10 @@
         return pl.pallas_call(
             make_kernel(leaf_n, share, strip),
             out_shape=jax.ShapeDtypeStruct(block.shape, f32),
-            in_specs=[pl.BlockSpec(memory_space=pltpu.VMEM)],
+            in_specs=[pl.BlockSpec(memory_space=pl.ANY)],
             out_specs=pl.BlockSpec(memory_space=pl.ANY),
             scratch_shapes=[
+                pltpu.VMEM(block.shape, f32),
                 pltpu.VMEM((6, wide, wide), f32),
                 pltpu.VMEM((2, 42, leaf_n // 3, leaf_n // 3), f32),
                 pltpu.VMEM((leaf_n, leaf_n), f32),
@@ -464,6 +469,7 @@
                 pltpu.SemaphoreType.DMA((ROUNDS,)),
                 pltpu.SemaphoreType.DMA((2 * SIDE,)),
                 pltpu.SemaphoreType.DMA((SIDE, 2)),
+                pltpu.SemaphoreType.DMA((1,)),
             ],
             compiler_params=pltpu.CompilerParams(
                 collective_id=0, has_side_effects=True, vmem_limit_bytes=60 * 2**20),

time: 123 us -> 122 us (level)
  the two profiles are of different devices: /device:TPU:100 before, /device:TPU:99 now
where the time goes in v2:
time: 122 us
  Pallas kernels  119 us (98%)
  local copies, waits for them, and re-layouts  2.36 us (2%)
    pallas_call x1, Pallas kernels, local_fn(): pl.pallas_call(make_kernel(leaf_n, share, strip), out_shape=jax.ShapeDtyp...  119 us

profile of v2, /device:TPU:99, one launch (start us, length us, event | category | flops | bytes accessed | tf_op | source)
XLA Modules:
  0.0 121.7 jit_solution(2476893524917283599)
XLA Ops:
  0.0 119.4 %spd_inverse.1 = f32[384,768]{1,0:T(8,128)} custom-call(f32[384,768]{1,0:T(8,128)} %block.1), custom_call_target="tpu_custom_call" | custom-call | tf_op jit(solution)/shard_map/spd_inverse/pallas_call | solution.py:450
  119.4 2.4 %copy.3 = f32[384,768]{1,0:T(8,128)} copy(f32[384,768]{1,0:T(8,128)} %spd_inverse.1) | data formatting | bytes 2359296
